TPU v7x, 512 devices: a whole 4x8x8 slice. The times are simulated.
512 devices in a mesh: seq: 8 (over z), mp: 16 (over y, core), dp: 4 (over x).
Axes of the slice: x: 4, y: 8, z: 8, core: 2. Of those that a mesh axis runs over, the one named last changes fastest.
Arguments:
- tokens: bfloat16 [65536, 2048], P(('dp', 'seq'), 'mp'), parts along dimension 0, may hold values from -6 to 6
- w_query: bfloat16 [2048, 2048], P(None, 'mp'), may hold values from -0.125 to 0.125
- w_key: bfloat16 [2048, 2048], P(None, 'mp'), may hold values from -0.125 to 0.125
- w_value: bfloat16 [2048, 2048], P(None, 'mp'), may hold values from -0.125 to 0.125
- w_gate: bfloat16 [2048, 2048], P(None, 'mp'), may hold values from -0.125 to 0.125
- decay_exponent: int32 [16], P('mp'), may hold values from 5 to 16
- forget: float32 [65536, 16], P(('dp', 'seq'), 'mp'), parts along dimension 0, may hold values from 0 to 0.69
- norm_gain: float32 [2048], replicated, may hold values from 0.1 to 1.9
Outputs:
- retained: bfloat16 [65536, 2048], P(('dp', 'seq', 'mp')), parts along dimension 0
There are 4 independent parts, one for each index of `dp`. A program takes and returns all parts, laid end to end along the dimension named above; an argument that names none is the same for every part. Nothing has to cross between parts.
All inputs are finite; a program needn't handle non-finite values.
Results may differ from a plain program's by a relative error of at most 0.015.
Values may be sent and summed in bfloat16 or wider, within the bound.
A program may use at most 64 MiB of HBM per device.

v0:
```python
import jax
import jax.numpy as jnp
from jax import lax
from jax.sharding import PartitionSpec as P

HEADS = 16
DH = 128


def from_everyone(shard, axis):
    copies = jnp.broadcast_to(shard, (lax.axis_size(axis), *shard.shape))
    return lax.all_to_all(copies, axis, split_axis=0, concat_axis=0, tiled=True)


def collected_together(shard, axis):
    leaves = jax.tree.leaves(shard)
    sequence = sorted(range(len(leaves)), key=lambda k: -leaves[k].size)
    width = (1, *leaves[sequence[0]].shape)[-1]
    lines = [
        jnp.pad(leaves[k].reshape(-1), (0, -leaves[k].size % width)).reshape(-1, width)
        for k in sequence
    ]
    both, at, found = (from_everyone(jnp.concatenate(lines), axis), 0, {})
    for k, line in zip(sequence, lines):
        section = both[:, at : at + len(line)].reshape(len(both), -1)
        found[k] = section[:, : leaves[k].size].reshape(-1, *leaves[k].shape)
        at += len(line)
    numbers = iter(range(len(leaves)))
    return jax.tree.map(lambda _: found[next(numbers)], shard)


def folded_in_pairs(pieces, combine):
    while len(jax.tree.leaves(pieces)[0]) > 1:
        pieces = jax.vmap(combine)(
            *(jax.tree.map(lambda part: part[side::2], pieces) for side in (0, 1))
        )
    return jax.tree.map(lambda part: part[0], pieces)


def prefix_2(shard, axis, combine, identity):
    size, index = (lax.axis_size(axis), lax.axis_index(axis))
    passed = jnp.arange(size) < index

    def kept(part, zero, own):
        part = jnp.where(
            passed.reshape(-1, *(1 for _ in own.shape)),
            part.astype(own.dtype),
            jnp.asarray(zero, own.dtype),
        )
        return part

    pieces = collected_together(
        jax.tree.map(lambda part, kind: part.astype(kind), shard, (jnp.bfloat16, jnp.bfloat16)),
        axis,
    )
    return folded_in_pairs(jax.tree.map(kept, pieces, identity, shard), combine)


def over_copies(shard, axis):
    return from_everyone(shard, axis).sum(axis=0)


def run_blocks(queries, key_rows, values, logdecay, head_count, head_width):
    seq_rows = queries.shape[0]
    block_rows = 512
    block_count = seq_rows // block_rows

    def shaped(source):
        return source.reshape(block_count, block_rows, head_count, head_width)

    decays = logdecay.reshape(block_count, block_rows, head_count)
    position = lax.broadcasted_iota(jnp.int32, (block_rows, block_rows), 0)
    earlier = lax.broadcasted_iota(jnp.int32, (block_rows, block_rows), 1)
    causal = position >= earlier

    def advance(carried, pieces):
        kv_state, offset = carried
        query_blk, key_blk, value_blk, decay_blk = pieces
        running = jnp.cumsum(decay_blk, axis=0)
        heads_first = running.T
        log_gap = heads_first[:, :, None] - heads_first[:, None, :]
        decay_mask = jnp.where(causal[None], jnp.exp(jnp.where(causal[None], log_gap, 0.0)), 0.0)
        scores = jnp.einsum("tha,sha->hts", query_blk, key_blk, preferred_element_type=jnp.float32)
        scores = (scores * decay_mask).astype(jnp.bfloat16)
        inner = jnp.einsum("hts,shb->thb", scores, value_blk, preferred_element_type=jnp.float32)
        query_float = query_blk.astype(jnp.float32)
        earlier_part = jnp.einsum(
            "tha,hab->thb", query_float * jnp.exp(running)[:, :, None], kv_state
        )
        query_device = query_float * jnp.exp(running + offset[None, :])[:, :, None]
        key_scaled = key_blk.astype(jnp.float32) * jnp.exp(running[-1:] - running)[:, :, None]
        kv_state = jnp.exp(running[-1])[:, None, None] * kv_state + jnp.einsum(
            "sha,shb->hab", key_scaled, value_blk.astype(jnp.float32)
        )
        return ((kv_state, offset + running[-1]), (inner + earlier_part, query_device))

    initial = (
        jnp.zeros((head_count, head_width, head_width), jnp.float32),
        jnp.zeros((head_count,), jnp.float32),
    )
    final, outputs = lax.scan(
        advance, initial, (shaped(queries), shaped(key_rows), shaped(values), decays)
    )
    local_part = outputs[0].reshape(seq_rows, head_count, head_width)
    query_device = outputs[1].reshape(seq_rows, head_count, head_width)
    return (local_part, query_device, final[0], final[1])


def combine_states(before, after):
    return (before[0] * after[0], after[0][:, None, None] * before[1] + after[1])


def body(tokens, w_query, w_key, w_value, w_gate, decay_exponent, forget, norm_gain):
    seq_rows = tokens.shape[0]
    local_width = w_query.shape[1]
    head_count = decay_exponent.shape[0]
    head_width = local_width // head_count
    empty = jnp.zeros((seq_rows, local_width), jnp.float32)
    summed = (empty, empty, empty, empty)
    piece = lax.all_gather(tokens, "mp", axis=1, tiled=True)
    results = []
    for weight, partial_value in zip((w_query, w_key, w_value, w_gate), summed):
        results.append(jnp.dot(piece, weight, preferred_element_type=jnp.float32))
    projected = tuple(results)
    queries = projected[0].astype(jnp.bfloat16)
    key_rows = (projected[1] * DH ** (-0.5)).astype(jnp.bfloat16)
    values = projected[2].astype(jnp.bfloat16)
    gate = projected[3].astype(jnp.bfloat16)
    rate = jnp.log1p(-jnp.exp2(-decay_exponent.astype(jnp.float32)))
    logdecay = rate[None, :] - forget
    local_part, query_device, own_state, own_total = run_blocks(
        queries, key_rows, values, logdecay, head_count, head_width
    )
    prefix = prefix_2(
        (jnp.exp(own_total), own_state),
        "seq",
        combine_states,
        (jnp.ones_like(own_total), jnp.zeros_like(own_state)),
    )
    incoming = prefix[1]
    from_before = jnp.einsum("tha,hab->thb", query_device, incoming)
    output = (local_part + from_before).astype(jnp.bfloat16).reshape(seq_rows, local_width)
    output_float = output.astype(jnp.float32)
    squares = over_copies(jnp.sum(output_float * output_float, axis=1), "mp")
    rstd = lax.rsqrt(squares / (HEADS * DH) + 1e-06)
    gain_here = lax.dynamic_slice_in_dim(
        norm_gain, lax.axis_index("mp") * local_width, local_width, 0
    )
    gated = (
        jax.nn.silu(gate.astype(jnp.float32)) * output_float * rstd[:, None] * gain_here[None, :]
    )
    return lax.all_to_all(gated.astype(jnp.bfloat16), "mp", split_axis=0, concat_axis=1, tiled=True)


def solution(mesh):
    placed = (
        P(("dp", "seq"), "mp"),
        P(None, "mp"),
        P(None, "mp"),
        P(None, "mp"),
        P(None, "mp"),
        P("mp"),
        P(("dp", "seq"), "mp"),
        P(),
    )
    return jax.shard_map(
        body, mesh=mesh, in_specs=placed, out_specs=P(("dp", "seq", "mp"), None), check_vma=False
    )
```

profile of v0, /device:TPU:1, one launch (start us, length us, event | category | flops | bytes accessed | tf_op | source)
XLA Modules:
  0.0 194.3 jit_solution(12837014939397995423)
XLA Ops:
  6.5 0.7 all-gather.2.cloned.1.call-update
  8.0 0.7 broadcast_subtract_fusion
  8.7 76.1 %all-gather.2.cloned.1.call-done = bf16[2048,2048]{1,0:T(8,128)(2,1)} async-done(((bf16[2048,128]{1,0:T(8,128)(2,1)}), bf16[2048,2048]{1,0:T(8,128)(2,1)}) %all-gather.2.cloned.1.call-update) | async-done | bytes 8388624 | tf_op jit(solution)/shard_map/all_gather | solution.py:120
  84.8 5.9 %fusion.52 = bf16[2048,128]{1,0:T(8,128)(2,1)S(1)} fusion(bf16[2048,2048]{1,0:T(8,128)(2,1)} %all-gather.2.cloned.1.call-done, bf16[2048,128]{1,0:T(8,128)(2,1)S(1)} %copy-done), kind=kOutput, calls=%fused_computation.61 | convolution fusion | flops 1074266112 | bytes 9437184 | tf_op jit(solution)/shard_map/dot_general | solution.py:123
  90.7 3.3 %convolution_convert_fusion.1 = bf16[2048,128]{1,0:T(8,128)(2,1)} fusion(bf16[2048,2048]{1,0:T(8,128)(2,1)S(1)} %copy-done.1, bf16[2048,128]{1,0:T(8,128)(2,1)S(1)} %copy-done.2), kind=kOutput, calls=%fused_computation.57 | convolution fusion | flops 1074003968 | bytes 9437184 | tf_op jit(solution)/shard_map/dot_general | solution.py:123
  94.0 2.4 %convolution_convert_fusion = bf16[2048,128]{1,0:T(8,128)(2,1)S(1)} fusion(bf16[2048,2048]{1,0:T(8,128)(2,1)S(1)} %copy-done.1, bf16[2048,128]{1,0:T(8,128)(2,1)S(1)} %copy-done.3), kind=kOutput, calls=%fused_computation.56 | convolution fusion | flops 1074003968 | bytes 9437184 | tf_op jit(solution)/shard_map/dot_general | solution.py:123
  96.4 29.3 %while.18 = (s32[]{:T(128)}, f32[1,128,128]{2,1,0:T(8,128)S(1)}, f32[1]{0:T(128)}, f32[4,512,1,128]{3,1,0,2:T(8,128)S(1)}, bf16[4,512,1,128]{3,1,2,0:T(8,128)(2,...) while((s32[]{:T(128)}, f32[1,128,128]{2,1,0:T(8,128)S(1)}, ...), condition=%wide.region_3.4_spmd.clone.clone, body=%wide.region_0.3_spmd.clone.clone.sunk | while | flops 169935888 | bytes 3247952 | solution.py:101
  96.4 0.3 reduce-window.16
  96.7 0.2 slice_reduce_fusion.2
  97.2 0.6 slice.110
  97.8 0.6 slice.109
  99.6 0.3 convolution_bitcast_fusion.4
  99.9 1.5 fusion.91
  101.6 1.3 fusion.90
  102.9 0.8 fusion.92
  103.7 0.3 reduce-window.16
  104.5 0.6 slice.110
  105.1 0.6 slice.109
  106.9 0.3 convolution_bitcast_fusion.4
  107.3 1.5 fusion.91
  108.9 1.3 fusion.90
  110.2 0.8 fusion.92
  111.0 0.3 reduce-window.16
  111.8 0.6 slice.110
  112.4 0.6 slice.109
  114.3 0.3 convolution_bitcast_fusion.4
  114.6 1.5 fusion.91
  116.2 1.3 fusion.90
  117.5 0.8 fusion.92
  118.3 0.3 reduce-window.16
  119.1 0.6 slice.110
  119.7 0.6 slice.109
  121.6 0.3 convolution_bitcast_fusion.4
  121.9 1.5 fusion.91
  123.5 1.3 fusion.90
  124.8 0.8 fusion.92
  125.7 0.8 broadcast_in_dim.45
  126.5 4.0 %all-to-all-start = ((bf16[8,129,128]{2,1,0:T(8,128)(2,1)}), bf16[8,129,128]{2,1,0:T(8,128)(2,1)S(1)}, u32[]{:S(2)}, u32[]{:S(2)}) async-start(bf16[8,129,128]{2,1,0:T(8,128)(2,1)} %broadcast_in_dim.45), calls=%async_computation | async-start | bytes 557056 | tf_op jit(solution)/shard_map/all_to_all | solution.py:12
  130.5 12.5 %all-to-all-done = bf16[8,129,128]{2,1,0:T(8,128)(2,1)S(1)} async-done(((bf16[8,129,128]{2,1,0:T(8,128)(2,1)}), bf16[8,129,128]{2,1,0:T(8,128)(2,1)S(1)}, u32[]{:S(2)}, u32[]{:S(2)}) %all-to-all-start) | async-done | bytes 264224 | tf_op jit(solution)/shard_map/all_to_all | solution.py:12
  143.4 0.5 slice.63
  144.2 2.1 %multiply_reduce_fusion = (f32[2048]{0:T(1024)S(1)}, f32[2048,128]{1,0:T(8,128)S(1)}) fusion(f32[2048,1,128]{2,0,1:T(8,128)S(1)} %bitcast.167, bf16[2048,128]{1,0:T(8,128)(2,1)} %bitcast.171, f32[2,1,128,128]{3,2,1,0:T(8,128)S(1)} %slice_add_fusion.1, f32[]{:T(128)} %bitcast.12), kind=kOutput, calls=%fused_computation.65 | convolution fusion | flops 68450304 | bytes 2760708 | tf_op jit(solution)/shard_map/tha,hab->thb/dot_general | solution.py:141
  146.3 0.7 broadcast_in_dim.49
  147.0 4.9 %all-to-all-start.1 = ((f32[16,1,2048]{2,1,0:T(1,128)}), f32[16,1,2048]{2,1,0:T(1,128)S(1)}, u32[]{:S(2)}, u32[]{:S(2)}) async-start(f32[16,1,2048]{2,1,0:T(1,128)} %broadcast_in_dim.49), calls=%async_computation.1 | async-start | bytes 262144 | tf_op jit(solution)/shard_map/all_to_all | solution.py:12
  151.9 0.8 dynamic_slice.17
  152.7 8.1 %all-to-all-done.1 = f32[16,1,2048]{2,1,0:T(1,128)S(1)} async-done(((f32[16,1,2048]{2,1,0:T(1,128)}), f32[16,1,2048]{2,1,0:T(1,128)S(1)}, u32[]{:S(2)}, u32[]{:S(2)}) %all-to-all-start.1) | async-done | bytes 131104 | tf_op jit(solution)/shard_map/all_to_all | solution.py:12
  160.9 5.8 %multiply_convert_fusion = bf16[2048,128]{1,0:T(8,128)(2,1)S(1)} fusion(f32[2048,128]{1,0:T(8,128)S(1)} %get-tuple-element.204, bf16[2048,2048]{1,0:T(8,128)(2,1)} %all-gather.2.cloned.1.call-done, bf16[2048,128]{1,0:T(8,128)(2,1)} %param.14, f32[128]{0:T(128)S(1)} %dynamic_slice.17, f32[2048]{0:T(1024)S(1)} %add_rsqrt_fusion), kind=kOutput, calls=%fused_computation.64 | convolution fusion | flops 1076363264 | bytes 10494464 | tf_op jit(solution)/shard_map/dot_general | solution.py:123
  166.7 19.9 %all_to_all.30 = bf16[16,128,128]{2,1,0:T(8,128)(2,1)S(1)} all-to-all(bf16[16,128,128]{2,1,0:T(8,128)(2,1)S(1)} %bitcast.170), channel_id=1, replica_groups=mesh['seq'=8,'mp'=16,'dp'=4] {'mp'}, dimensions={0} | all-to-all | bytes 1048576 | tf_op jit(solution)/shard_map/all_to_all | solution.py:152
  186.6 0.9 copy_bitcast_fusion
  (65 shorter events, 3.3 us)
Async XLA Ops:
  6.5 78.2 %copy-start = (bf16[2048,128]{1,0:T(8,128)(2,1)S(1)}, bf16[2048,128]{1,0:T(8,128)(2,1)}, u32[]{:S(2)}) copy-start(bf16[2048,128]{1,0:T(8,128)(2,1)} %param.12) | copy-start | bytes 1572868
  6.5 84.1 %copy-start.2 = (bf16[2048,128]{1,0:T(8,128)(2,1)S(1)}, bf16[2048,128]{1,0:T(8,128)(2,1)}, u32[]{:S(2)}) copy-start(bf16[2048,128]{1,0:T(8,128)(2,1)} %param.13) | copy-start | bytes 1572868
  6.5 78.2 %all-gather.2.cloned.1.call-start = ((), (), s32[]{:S(2)}) async-start(), calls=%async_computation.3 | async-start | bytes 8912896 | tf_op jit(solution)/shard_map/all_gather | solution.py:120
  84.8 5.9 %copy-start.1 = (bf16[2048,2048]{1,0:T(8,128)(2,1)S(1)}, bf16[2048,2048]{1,0:T(8,128)(2,1)}, u32[]{:S(2)}) copy-start(bf16[2048,2048]{1,0:T(8,128)(2,1)} %all-gather.2.cloned.1.call-done) | copy-start | bytes 25165828
  90.7 3.3 %copy-start.3 = (bf16[2048,128]{1,0:T(8,128)(2,1)S(1)}, bf16[2048,128]{1,0:T(8,128)(2,1)}, u32[]{:S(2)}) copy-start(bf16[2048,128]{1,0:T(8,128)(2,1)} %param.11) | copy-start | bytes 1572868
  126.5 16.6 %all-to-all-start = ((bf16[8,129,128]{2,1,0:T(8,128)(2,1)}), bf16[8,129,128]{2,1,0:T(8,128)(2,1)S(1)}, u32[]{:S(2)}, u32[]{:S(2)}) async-start(bf16[8,129,128]{2,1,0:T(8,128)(2,1)} %broadcast_in_dim.45), calls=%async_computation | async-start | bytes 557056 | tf_op jit(solution)/shard_map/all_to_all | solution.py:12
  147.0 13.8 %all-to-all-start.1 = ((f32[16,1,2048]{2,1,0:T(1,128)}), f32[16,1,2048]{2,1,0:T(1,128)S(1)}, u32[]{:S(2)}, u32[]{:S(2)}) async-start(f32[16,1,2048]{2,1,0:T(1,128)} %broadcast_in_dim.49), calls=%async_computation.1 | async-start | bytes 262144 | tf_op jit(solution)/shard_map/all_to_all | solution.py:12
Sparse Core Ops, SparseCore 0:
  9.4 75.3 all-gather.1
where the time goes:
time: 195 us; the launch traced here: 194 us
  waiting for transfers between devices  97.4 us (50%)
  matrix products  31.5 us (16%)
  blocking collectives  19.9 us (10%)
  between operations  14.3 us (7%)
  local copies, waits for them, and re-layouts  10.2 us (5%)
  starting transfers between devices  8.92 us (5%)
  other arithmetic  6.83 us (4%)
  loops' own time  5.24 us (3%)
    all_gather x1, waiting for transfers between devices, body(): piece = lax.all_gather(tokens, 'mp', axis=1, tiled=True)  76.1 us
    all_to_all x2, waiting for transfers between devices, from_everyone(): return lax.all_to_all(copies, axis, split_axis=0, concat_axis=0, tiled=True)  20.7 us
    all_to_all x1, blocking collectives, body(): lax.all_to_all(gated.astype(jnp.bfloat16), 'mp', split_axis=0, concat_axi...  19.9 us
    dot_general x4, matrix products, body(): results.append(jnp.dot(piece, weight, preferred_element_type=jnp.float32))  17.3 us
    all_to_all x2, starting transfers between devices, from_everyone(): return lax.all_to_all(copies, axis, split_axis=0, concat_axis=0, tiled=True)  8.92 us
    dot_general x4, matrix products, advance(): jnp.einsum('hts,shb->thb', scores, value_blk, preferred_element_type=jnp....  5.87 us
    another operation x1, loops' own time, run_blocks(): lax.scan(advance, initial, (shaped(queries), shaped(key_rows), shaped(val...  5.24 us
    dot_general x4, matrix products, advance(): jnp.einsum('sha,shb->hab', key_scaled, value_blk.astype(jnp.float32))  5.01 us
  transfers between devices with their start and end apart: 3, of which 3 were waited for; matrix products, arithmetic and copies ran while one was open for 1% of the time, Pallas kernels for 0%

commit v1 on v0

--- a/solution.py
+++ b/solution.py
@@ -117,7 +117,20 @@
     head_width = local_width // head_count
     empty = jnp.zeros((seq_rows, local_width), jnp.float32)
     summed = (empty, empty, empty, empty)
-    piece = lax.all_gather(tokens, "mp", axis=1, tiled=True)
+    ways, here, step = (lax.axis_size("mp"), lax.axis_index("mp"), tokens.shape[1])
+    dims = [n * ways if d == 1 else n for d, n in enumerate(tokens.shape)]
+    piece = lax.dynamic_update_slice_in_dim(
+        jnp.zeros(dims, tokens.dtype), tokens, here * step, axis=1
+    )
+    going_up = going_down = tokens
+    for far in range(1, ways // 2 + 1):
+        going_up = lax.ppermute(going_up, "mp", [(d, (d + 1) % ways) for d in range(ways)])
+        piece = lax.dynamic_update_slice_in_dim(piece, going_up, (here - far) % ways * step, axis=1)
+        if 2 * far < ways:
+            going_down = lax.ppermute(going_down, "mp", [(d, (d - 1) % ways) for d in range(ways)])
+            piece = lax.dynamic_update_slice_in_dim(
+                piece, going_down, (here + far) % ways * step, axis=1
+            )
     results = []
     for weight, partial_value in zip((w_query, w_key, w_value, w_gate), summed):
         results.append(jnp.dot(piece, weight, preferred_element_type=jnp.float32))

time: 195 us -> 201 us (1.031)
  waiting for transfers between devices: 97.4 us -> 26.5 us
  starting transfers between devices: 8.92 us -> 68.9 us
  local copies, waits for them, and re-layouts: 10.2 us -> 33.5 us
  between operations: 14.3 us -> 0.93 us
  matrix products: 31.5 us -> 38.1 us
    all_gather x1 -> x0, waiting for transfers between devices: 76.1 us -> none  [body(): piece = lax.all_gather(tokens, 'mp', axis=1, tiled=True)]
    ppermute x0 -> x15, starting transfers between devices: none -> 47.8 us  [the longest x7 39.3 us: body(): lax.ppermute(going_down, 'mp', [(d, (d - 1) % ways) for d in range(ways)])]
    dynamic_update_slice x0 -> x16, local copies, waits for them, and re-layouts: none -> 18.6 us  [the longest x8 9.22 us: body(): lax.dynamic_update_slice_in_dim(piece, going_up, (here - far) % ways * st...]
    all_to_all x2, starting transfers between devices: 8.92 us -> 21 us  [from_everyone(): return lax.all_to_all(copies, axis, split_axis=0, concat_axis=0, tiled=True)]
    ppermute x0 -> x15, waiting for transfers between devices: none -> 8.9 us  [the longest x8 7.23 us: body(): lax.ppermute(going_up, 'mp', [(d, (d + 1) % ways) for d in range(ways)])]
    dot_general x4, matrix products: 17.3 us -> 23.9 us  [body(): results.append(jnp.dot(piece, weight, preferred_element_type=jnp.float32))]
    broadcast_in_dim x0 -> x1, local copies, waits for them, and re-layouts: none -> 4.29 us  [body(): jnp.zeros(dims, tokens.dtype)]
    all_to_all x2, waiting for transfers between devices: 20.7 us -> 17.6 us  [from_everyone(): return lax.all_to_all(copies, axis, split_axis=0, concat_axis=0, tiled=True)]
  transfers between devices with their start and end apart: 3 -> 17, of which waited for: 3 -> 7; matrix products, arithmetic and copies ran while one was open for 1% -> 12% of each run, Pallas kernels for 0% -> 0%
where the time goes in v1:
time: 201 us; the launch traced here: 200 us
  starting transfers between devices  68.9 us (34%)
  matrix products  38.1 us (19%)
  local copies, waits for them, and re-layouts  33.5 us (17%)
  waiting for transfers between devices  26.5 us (13%)
  blocking collectives  19.9 us (10%)
  other arithmetic  6.83 us (3%)
  loops' own time  5.66 us (3%)
    ppermute x7, starting transfers between devices, body(): lax.ppermute(going_down, 'mp', [(d, (d - 1) % ways) for d in range(ways)])  39.3 us
    dot_general x4, matrix products, body(): results.append(jnp.dot(piece, weight, preferred_element_type=jnp.float32))  23.9 us
    all_to_all x2, starting transfers between devices, from_everyone(): return lax.all_to_all(copies, axis, split_axis=0, concat_axis=0, tiled=True)  21 us
    all_to_all x1, blocking collectives, body(): lax.all_to_all(gated.astype(jnp.bfloat16), 'mp', split_axis=0, concat_axi...  19.9 us
    all_to_all x2, waiting for transfers between devices, from_everyone(): return lax.all_to_all(copies, axis, split_axis=0, concat_axis=0, tiled=True)  17.6 us
    dynamic_update_slice x8, local copies, waits for them, and re-layouts, body(): lax.dynamic_update_slice_in_dim(piece, going_up, (here - far) % ways * st...  9.22 us
    ppermute x8, starting transfers between devices, body(): lax.ppermute(going_up, 'mp', [(d, (d + 1) % ways) for d in range(ways)])  8.48 us
    dynamic_update_slice x7, local copies, waits for them, and re-layouts, body(): lax.dynamic_update_slice_in_dim(piece, going_down, (here + far) % ways *...  8.43 us
  transfers between devices with their start and end apart: 17, of which 7 were waited for; matrix products, arithmetic and copies ran while one was open for 12% of the time, Pallas kernels for 0%

profile of v1, /device:TPU:1, one launch (start us, length us, event | category | flops | bytes accessed | tf_op | source)
XLA Modules:
  0.0 200.3 jit_solution(5323872683217348478)
XLA Ops:
  0.0 2.7 %collective-permute-start = (bf16[2048,128]{1,0:T(8,128)(2,1)}, bf16[2048,128]{1,0:T(8,128)(2,1)S(1)}, u32[]{:S(2)}, u32[]{:S(2)}) collective-permute-start(bf16[2048,128]{1,0:T(8,128)(2,1)} %param.10), channel_id=1, source_target_pairs={{0,4},{4,8},{8,12},{12,16},{16,20},{20,24},{24,28},{28,32},{32,36}... | collective-permute-start | bytes 1572872 | tf_op jit(solution)/shard_map/ppermute | solution.py:127
  2.7 4.2 %collective-permute-start.1 = (bf16[2048,128]{1,0:T(8,128)(2,1)}, bf16[2048,128]{1,0:T(8,128)(2,1)S(1)}, u32[]{:S(2)}, u32[]{:S(2)}) collective-permute-start(bf16[2048,128]{1,0:T(8,128)(2,1)} %param.10), channel_id=1, source_target_pairs={{0,60},{4,0},{8,4},{12,8},{16,12},{20,16},{24,20},{28,24},{32,28},... | collective-permute-start | bytes 1572872 | tf_op jit(solution)/shard_map/ppermute | solution.py:130
  6.8 2.8 %collective-permute-done = bf16[2048,128]{1,0:T(8,128)(2,1)S(1)} collective-permute-done((bf16[2048,128]{1,0:T(8,128)(2,1)}, bf16[2048,128]{1,0:T(8,128)(2,1)S(1)}, u32[]{:S(2)}, u32[]{:S(2)}) %collective-permute-start) | collective-permute-done | bytes 524320 | tf_op jit(solution)/shard_map/ppermute | solution.py:127
  9.7 2.4 %collective-permute-start.2 = (bf16[2048,128]{1,0:T(8,128)(2,1)S(1)}, bf16[2048,128]{1,0:T(8,128)(2,1)S(1)}, u32[]{:S(2)}, u32[]{:S(2)}) collective-permute-start(bf16[2048,128]{1,0:T(8,128)(2,1)S(1)} %collective-permute-done), channel_id=1, source_target_pairs={{0,4},{4,8},{8,12},{12,16},{16,20},{20,24},{24,28},{28,32},{32,36}... | collective-permute-start | bytes 1572872 | tf_op jit(solution)/shard_map/ppermute | solution.py:127
  12.0 4.9 %collective-permute-start.3 = (bf16[2048,128]{1,0:T(8,128)(2,1)S(1)}, bf16[2048,128]{1,0:T(8,128)(2,1)S(1)}, u32[]{:S(2)}, u32[]{:S(2)}) collective-permute-start(bf16[2048,128]{1,0:T(8,128)(2,1)S(1)} %collective-permute-done.1), channel_id=1, source_target_pairs={{0,60},{4,0},{8,4},{12,8},{16,12},{20,16},{24,20},{28,24},{32,28},... | collective-permute-start | bytes 1572872 | tf_op jit(solution)/shard_map/ppermute | solution.py:130
  16.9 1.4 collective-permute-done.2
  18.3 2.4 %collective-permute-start.4 = (bf16[2048,128]{1,0:T(8,128)(2,1)S(1)}, bf16[2048,128]{1,0:T(8,128)(2,1)S(1)}, u32[]{:S(2)}, u32[]{:S(2)}) collective-permute-start(bf16[2048,128]{1,0:T(8,128)(2,1)S(1)} %collective-permute-done.2), channel_id=1, source_target_pairs={{0,4},{4,8},{8,12},{12,16},{16,20},{20,24},{24,28},{28,32},{32,36}... | collective-permute-start | bytes 1572872 | tf_op jit(solution)/shard_map/ppermute | solution.py:127
  21.4 6.1 %collective-permute-start.5 = (bf16[2048,128]{1,0:T(8,128)(2,1)S(1)}, bf16[2048,128]{1,0:T(8,128)(2,1)}, u32[]{:S(2)}, u32[]{:S(2)}) collective-permute-start(bf16[2048,128]{1,0:T(8,128)(2,1)S(1)} %collective-permute-done.3), channel_id=1, source_target_pairs={{0,60},{4,0},{8,4},{12,8},{16,12},{20,16},{24,20},{28,24},{32,28},... | collective-permute-start | bytes 1572872 | tf_op jit(solution)/shard_map/ppermute | solution.py:130
  28.2 1.1 collective-permute-start.6
  29.2 4.3 %broadcast_in_dim.48 = bf16[2048,2048]{1,0:T(8,128)(2,1)} broadcast(bf16[]{:T(256)} %constant.127.clone.1), dimensions={} | broadcast | bytes 8388610 | tf_op jit(solution)/shard_map/broadcast_in_dim | solution.py:123
  33.5 0.9 constant_dynamic-update-slice_fusion.16
  34.4 1.9 constant_dynamic-update-slice_fusion.15
  36.4 7.3 %collective-permute-start.7 = (bf16[2048,128]{1,0:T(8,128)(2,1)}, bf16[2048,128]{1,0:T(8,128)(2,1)S(1)}, u32[]{:S(2)}, u32[]{:S(2)}) collective-permute-start(bf16[2048,128]{1,0:T(8,128)(2,1)} %collective-permute-done.5), channel_id=1, source_target_pairs={{0,60},{4,0},{8,4},{12,8},{16,12},{20,16},{24,20},{28,24},{32,28},... | collective-permute-start | bytes 1572872 | tf_op jit(solution)/shard_map/ppermute | solution.py:130
  43.6 2.0 constant_dynamic-update-slice_fusion.14
  45.6 0.9 constant_dynamic-update-slice_fusion.13
  46.5 0.9 constant_dynamic-update-slice_fusion.12
  47.4 6.2 %collective-permute-start.9 = (bf16[2048,128]{1,0:T(8,128)(2,1)S(1)}, bf16[2048,128]{1,0:T(8,128)(2,1)S(1)}, u32[]{:S(2)}, u32[]{:S(2)}) collective-permute-start(bf16[2048,128]{1,0:T(8,128)(2,1)S(1)} %collective-permute-done.7), channel_id=1, source_target_pairs={{0,60},{4,0},{8,4},{12,8},{16,12},{20,16},{24,20},{28,24},{32,28},... | collective-permute-start | bytes 1572872 | tf_op jit(solution)/shard_map/ppermute | solution.py:130
  53.6 0.9 constant_dynamic-update-slice_fusion.11
  54.5 1.9 constant_dynamic-update-slice_fusion.10
  56.5 1.9 constant_dynamic-update-slice_fusion.9
  58.4 4.9 %collective-permute-start.11 = (bf16[2048,128]{1,0:T(8,128)(2,1)S(1)}, bf16[2048,128]{1,0:T(8,128)(2,1)S(1)}, u32[]{:S(2)}, u32[]{:S(2)}) collective-permute-start(bf16[2048,128]{1,0:T(8,128)(2,1)S(1)} %collective-permute-done.9), channel_id=1, source_target_pairs={{0,60},{4,0},{8,4},{12,8},{16,12},{20,16},{24,20},{28,24},{32,28},... | collective-permute-start | bytes 1572872 | tf_op jit(solution)/shard_map/ppermute | solution.py:130
  63.3 0.9 constant_dynamic-update-slice_fusion.8
  65.2 0.9 constant_dynamic-update-slice_fusion.6
  66.1 1.3 collective-permute-done.11
  67.3 5.8 %collective-permute-start.13 = (bf16[2048,128]{1,0:T(8,128)(2,1)S(1)}, bf16[2048,128]{1,0:T(8,128)(2,1)S(1)}, u32[]{:S(2)}, u32[]{:S(2)}) collective-permute-start(bf16[2048,128]{1,0:T(8,128)(2,1)S(1)} %collective-permute-done.11), channel_id=1, source_target_pairs={{0,60},{4,0},{8,4},{12,8},{16,12},{20,16},{24,20},{28,24},{32,28},... | collective-permute-start | bytes 1572872 | tf_op jit(solution)/shard_map/ppermute | solution.py:130
  74.9 0.9 constant_dynamic-update-slice_fusion.3
  76.2 0.9 constant_dynamic-update-slice_fusion.2
  77.1 3.0 %collective-permute-done.14 = bf16[2048,128]{1,0:T(8,128)(2,1)S(1)} collective-permute-done((bf16[2048,128]{1,0:T(8,128)(2,1)S(1)}, bf16[2048,128]{1,0:T(8,128)(2,1)S(1)}, u32[]{:S(2)}, u32[]{:S(2)}) %collective-permute-start.14) | collective-permute-done | bytes 524320 | tf_op jit(solution)/shard_map/ppermute | solution.py:127
  80.2 0.9 constant_dynamic-update-slice_fusion.1
  81.1 5.7 %fusion.52 = bf16[2048,128]{1,0:T(8,128)(2,1)S(1)} fusion(bf16[2048,2048]{1,0:T(8,128)(2,1)} %constant_dynamic-update-slice_fusion.1, bf16[2048,128]{1,0:T(8,128)(2,1)S(1)} %copy-done), kind=kOutput, calls=%fused_computation.61 | convolution fusion | flops 1074266112 | bytes 9437184 | tf_op jit(solution)/shard_map/dot_general | solution.py:136
  86.8 6.6 %convolution_convert_fusion.1 = bf16[2048,128]{1,0:T(8,128)(2,1)} fusion(bf16[2048,2048]{1,0:T(8,128)(2,1)} %constant_dynamic-update-slice_fusion.1, bf16[2048,128]{1,0:T(8,128)(2,1)S(1)} %copy-done.4), kind=kOutput, calls=%fused_computation.57 | convolution fusion | flops 1074003968 | bytes 9437184 | tf_op jit(solution)/shard_map/dot_general | solution.py:136
  93.5 5.7 %convolution_convert_fusion = bf16[2048,128]{1,0:T(8,128)(2,1)S(1)} fusion(bf16[2048,2048]{1,0:T(8,128)(2,1)} %constant_dynamic-update-slice_fusion.1, bf16[2048,128]{1,0:T(8,128)(2,1)S(1)} %copy-done.5), kind=kOutput, calls=%fused_computation.56 | convolution fusion | flops 1074003968 | bytes 9437184 | tf_op jit(solution)/shard_map/dot_general | solution.py:136
  99.2 30.1 %while.18 = (s32[]{:T(128)}, f32[1,128,128]{2,1,0:T(8,128)S(1)}, f32[1]{0:T(128)}, f32[4,512,1,128]{3,1,0,2:T(8,128)S(1)}, bf16[4,512,1,128]{3,1,2,0:T(8,128)(2,...) while((s32[]{:T(128)}, f32[1,128,128]{2,1,0:T(8,128)S(1)}, ...), condition=%wide.region_3.4_spmd.clone.clone, body=%wide.region_0.3_spmd.clone.clone.sunk | while | flops 169935888 | bytes 3247952 | solution.py:101
  103.0 1.5 fusion.91
  104.7 1.3 fusion.90
  110.5 1.5 fusion.91
  112.2 1.3 fusion.90
  118.0 1.5 fusion.91
  119.7 1.3 fusion.90
  125.5 1.5 fusion.91
  127.2 1.3 fusion.90
  130.1 4.7 %all-to-all-start = ((bf16[8,129,128]{2,1,0:T(8,128)(2,1)}), bf16[8,129,128]{2,1,0:T(8,128)(2,1)S(1)}, u32[]{:S(2)}, u32[]{:S(2)}) async-start(bf16[8,129,128]{2,1,0:T(8,128)(2,1)} %broadcast_in_dim.49), calls=%async_computation | async-start | bytes 557056 | tf_op jit(solution)/shard_map/all_to_all | solution.py:12
  134.8 9.5 %all-to-all-done = bf16[8,129,128]{2,1,0:T(8,128)(2,1)S(1)} async-done(((bf16[8,129,128]{2,1,0:T(8,128)(2,1)}), bf16[8,129,128]{2,1,0:T(8,128)(2,1)S(1)}, u32[]{:S(2)}, u32[]{:S(2)}) %all-to-all-start) | async-done | bytes 264224 | tf_op jit(solution)/shard_map/all_to_all | solution.py:12
  145.6 2.2 %multiply_reduce_fusion = (f32[2048]{0:T(1024)S(1)}, f32[2048,128]{1,0:T(8,128)S(1)}) fusion(f32[2048,1,128]{2,0,1:T(8,128)S(1)} %bitcast.167, bf16[2048,128]{1,0:T(8,128)(2,1)} %bitcast.171, f32[2,1,128,128]{3,2,1,0:T(8,128)S(1)} %slice_add_fusion.1, f32[]{:T(128)} %bitcast.12), kind=kOutput, calls=%fused_computation.65 | convolution fusion | flops 68450304 | bytes 2760708 | tf_op jit(solution)/shard_map/tha,hab->thb/dot_general | solution.py:154
  148.5 16.3 %all-to-all-start.1 = ((f32[16,1,2048]{2,1,0:T(1,128)}), f32[16,1,2048]{2,1,0:T(1,128)S(1)}, u32[]{:S(2)}, u32[]{:S(2)}) async-start(f32[16,1,2048]{2,1,0:T(1,128)} %broadcast_in_dim.53), calls=%async_computation.1 | async-start | bytes 262144 | tf_op jit(solution)/shard_map/all_to_all | solution.py:12
  165.6 8.1 %all-to-all-done.1 = f32[16,1,2048]{2,1,0:T(1,128)S(1)} async-done(((f32[16,1,2048]{2,1,0:T(1,128)}), f32[16,1,2048]{2,1,0:T(1,128)S(1)}, u32[]{:S(2)}, u32[]{:S(2)}) %all-to-all-start.1) | async-done | bytes 131104 | tf_op jit(solution)/shard_map/all_to_all | solution.py:12
  173.8 5.8 %multiply_convert_fusion = bf16[2048,128]{1,0:T(8,128)(2,1)S(1)} fusion(f32[2048,128]{1,0:T(8,128)S(1)} %get-tuple-element.204, bf16[2048,2048]{1,0:T(8,128)(2,1)} %constant_dynamic-update-slice_fusion.1, bf16[2048,128]{1,0:T(8,128)(2,1)} %param.14, f32[128]{0:T(128)S(1)} %dynamic_slice.17, f32[2048]{0:T(1024)S(1)} %add_rsqrt_fusion), kind=kOutput, calls=%fused_computation.64 | convolution fusion | flops 1076363264 | bytes 10494464 | tf_op jit(solution)/shard_map/dot_general | solution.py:136
  179.6 19.9 %all_to_all.30 = bf16[16,128,128]{2,1,0:T(8,128)(2,1)S(1)} all-to-all(bf16[16,128,128]{2,1,0:T(8,128)(2,1)S(1)} %bitcast.170), channel_id=1, replica_groups=mesh['seq'=8,'mp'=16,'dp'=4] {'mp'}, dimensions={0} | all-to-all | bytes 1048576 | tf_op jit(solution)/shard_map/all_to_all | solution.py:165
  (113 shorter events, 21.8 us)
Async XLA Ops:
  0.0 81.1 %copy-start = (bf16[2048,128]{1,0:T(8,128)(2,1)S(1)}, bf16[2048,128]{1,0:T(8,128)(2,1)}, u32[]{:S(2)}) copy-start(bf16[2048,128]{1,0:T(8,128)(2,1)} %param.12) | copy-start | bytes 1572868
  0.0 33.5 %copy-start.1 = (bf16[2048,128]{1,0:T(8,128)(2,1)S(1)}, bf16[2048,128]{1,0:T(8,128)(2,1)}, u32[]{:S(2)}) copy-start(bf16[2048,128]{1,0:T(8,128)(2,1)} %param.10) | copy-start | bytes 1572868
  0.0 9.6 %collective-permute-start = (bf16[2048,128]{1,0:T(8,128)(2,1)}, bf16[2048,128]{1,0:T(8,128)(2,1)S(1)}, u32[]{:S(2)}, u32[]{:S(2)}) collective-permute-start(bf16[2048,128]{1,0:T(8,128)(2,1)} %param.10), channel_id=1, source_target_pairs={{0,4},{4,8},{8,12},{12,16},{16,20},{20,24},{24,28},{28,32},{32,36}... | collective-permute-start | bytes 1572872 | tf_op jit(solution)/shard_map/ppermute | solution.py:127
  2.7 9.3 %collective-permute-start.1 = (bf16[2048,128]{1,0:T(8,128)(2,1)}, bf16[2048,128]{1,0:T(8,128)(2,1)S(1)}, u32[]{:S(2)}, u32[]{:S(2)}) collective-permute-start(bf16[2048,128]{1,0:T(8,128)(2,1)} %param.10), channel_id=1, source_target_pairs={{0,60},{4,0},{8,4},{12,8},{16,12},{20,16},{24,20},{28,24},{32,28},... | collective-permute-start | bytes 1572872 | tf_op jit(solution)/shard_map/ppermute | solution.py:130
  9.6 7.3 %copy-start.3 = (bf16[2048,128]{1,0:T(8,128)(2,1)}, bf16[2048,128]{1,0:T(8,128)(2,1)S(1)}, u32[]{:S(2)}) copy-start(bf16[2048,128]{1,0:T(8,128)(2,1)S(1)} %collective-permute-done) | copy-start | bytes 1572868
  9.7 8.6 %collective-permute-start.2 = (bf16[2048,128]{1,0:T(8,128)(2,1)S(1)}, bf16[2048,128]{1,0:T(8,128)(2,1)S(1)}, u32[]{:S(2)}, u32[]{:S(2)}) collective-permute-start(bf16[2048,128]{1,0:T(8,128)(2,1)S(1)} %collective-permute-done), channel_id=1, source_target_pairs={{0,4},{4,8},{8,12},{12,16},{16,20},{20,24},{24,28},{28,32},{32,36}... | collective-permute-start | bytes 1572872 | tf_op jit(solution)/shard_map/ppermute | solution.py:127
  12.0 9.4 %copy-start.2 = (bf16[2048,128]{1,0:T(8,128)(2,1)}, bf16[2048,128]{1,0:T(8,128)(2,1)S(1)}, u32[]{:S(2)}) copy-start(bf16[2048,128]{1,0:T(8,128)(2,1)S(1)} %collective-permute-done.1) | copy-start | bytes 1572868
  12.0 9.3 %collective-permute-start.3 = (bf16[2048,128]{1,0:T(8,128)(2,1)S(1)}, bf16[2048,128]{1,0:T(8,128)(2,1)S(1)}, u32[]{:S(2)}, u32[]{:S(2)}) collective-permute-start(bf16[2048,128]{1,0:T(8,128)(2,1)S(1)} %collective-permute-done.1), channel_id=1, source_target_pairs={{0,60},{4,0},{8,4},{12,8},{16,12},{20,16},{24,20},{28,24},{32,28},... | collective-permute-start | bytes 1572872 | tf_op jit(solution)/shard_map/ppermute | solution.py:130
  18.3 9.9 %collective-permute-start.4 = (bf16[2048,128]{1,0:T(8,128)(2,1)S(1)}, bf16[2048,128]{1,0:T(8,128)(2,1)S(1)}, u32[]{:S(2)}, u32[]{:S(2)}) collective-permute-start(bf16[2048,128]{1,0:T(8,128)(2,1)S(1)} %collective-permute-done.2), channel_id=1, source_target_pairs={{0,4},{4,8},{8,12},{12,16},{16,20},{20,24},{24,28},{28,32},{32,36}... | collective-permute-start | bytes 1572872 | tf_op jit(solution)/shard_map/ppermute | solution.py:127
  21.4 15.0 %collective-permute-start.5 = (bf16[2048,128]{1,0:T(8,128)(2,1)S(1)}, bf16[2048,128]{1,0:T(8,128)(2,1)}, u32[]{:S(2)}, u32[]{:S(2)}) collective-permute-start(bf16[2048,128]{1,0:T(8,128)(2,1)S(1)} %collective-permute-done.3), channel_id=1, source_target_pairs={{0,60},{4,0},{8,4},{12,8},{16,12},{20,16},{24,20},{28,24},{32,28},... | collective-permute-start | bytes 1572872 | tf_op jit(solution)/shard_map/ppermute | solution.py:130
  28.2 17.4 %collective-permute-start.6 = (bf16[2048,128]{1,0:T(8,128)(2,1)S(1)}, bf16[2048,128]{1,0:T(8,128)(2,1)}, u32[]{:S(2)}, u32[]{:S(2)}) collective-permute-start(bf16[2048,128]{1,0:T(8,128)(2,1)S(1)} %collective-permute-done.4), channel_id=1, source_target_pairs={{0,4},{4,8},{8,12},{12,16},{16,20},{20,24},{24,28},{28,32},{32,36}... | collective-permute-start | bytes 1572872 | tf_op jit(solution)/shard_map/ppermute | solution.py:127
  36.4 11.1 %collective-permute-start.7 = (bf16[2048,128]{1,0:T(8,128)(2,1)}, bf16[2048,128]{1,0:T(8,128)(2,1)S(1)}, u32[]{:S(2)}, u32[]{:S(2)}) collective-permute-start(bf16[2048,128]{1,0:T(8,128)(2,1)} %collective-permute-done.5), channel_id=1, source_target_pairs={{0,60},{4,0},{8,4},{12,8},{16,12},{20,16},{24,20},{28,24},{32,28},... | collective-permute-start | bytes 1572872 | tf_op jit(solution)/shard_map/ppermute | solution.py:130
  45.6 8.9 %collective-permute-start.8 = (bf16[2048,128]{1,0:T(8,128)(2,1)}, bf16[2048,128]{1,0:T(8,128)(2,1)S(1)}, u32[]{:S(2)}, u32[]{:S(2)}) collective-permute-start(bf16[2048,128]{1,0:T(8,128)(2,1)} %collective-permute-done.6), channel_id=1, source_target_pairs={{0,4},{4,8},{8,12},{12,16},{16,20},{20,24},{24,28},{28,32},{32,36}... | collective-permute-start | bytes 1572872 | tf_op jit(solution)/shard_map/ppermute | solution.py:127
  47.4 11.0 %collective-permute-start.9 = (bf16[2048,128]{1,0:T(8,128)(2,1)S(1)}, bf16[2048,128]{1,0:T(8,128)(2,1)S(1)}, u32[]{:S(2)}, u32[]{:S(2)}) collective-permute-start(bf16[2048,128]{1,0:T(8,128)(2,1)S(1)} %collective-permute-done.7), channel_id=1, source_target_pairs={{0,60},{4,0},{8,4},{12,8},{16,12},{20,16},{24,20},{28,24},{32,28},... | collective-permute-start | bytes 1572872 | tf_op jit(solution)/shard_map/ppermute | solution.py:130
  54.5 9.8 %collective-permute-start.10 = (bf16[2048,128]{1,0:T(8,128)(2,1)S(1)}, bf16[2048,128]{1,0:T(8,128)(2,1)S(1)}, u32[]{:S(2)}, u32[]{:S(2)}) collective-permute-start(bf16[2048,128]{1,0:T(8,128)(2,1)S(1)} %collective-permute-done.8), channel_id=1, source_target_pairs={{0,4},{4,8},{8,12},{12,16},{16,20},{20,24},{24,28},{28,32},{32,36}... | collective-permute-start | bytes 1572872 | tf_op jit(solution)/shard_map/ppermute | solution.py:127
  58.4 8.9 %collective-permute-start.11 = (bf16[2048,128]{1,0:T(8,128)(2,1)S(1)}, bf16[2048,128]{1,0:T(8,128)(2,1)S(1)}, u32[]{:S(2)}, u32[]{:S(2)}) collective-permute-start(bf16[2048,128]{1,0:T(8,128)(2,1)S(1)} %collective-permute-done.9), channel_id=1, source_target_pairs={{0,60},{4,0},{8,4},{12,8},{16,12},{20,16},{24,20},{28,24},{32,28},... | collective-permute-start | bytes 1572872 | tf_op jit(solution)/shard_map/ppermute | solution.py:130
  64.3 9.8 %collective-permute-start.12 = (bf16[2048,128]{1,0:T(8,128)(2,1)S(1)}, bf16[2048,128]{1,0:T(8,128)(2,1)S(1)}, u32[]{:S(2)}, u32[]{:S(2)}) collective-permute-start(bf16[2048,128]{1,0:T(8,128)(2,1)S(1)} %collective-permute-done.10), channel_id=1, source_target_pairs={{0,4},{4,8},{8,12},{12,16},{16,20},{20,24},{24,28},{28,32},{32,36}... | collective-permute-start | bytes 1572872 | tf_op jit(solution)/shard_map/ppermute | solution.py:127
  67.3 8.9 %collective-permute-start.13 = (bf16[2048,128]{1,0:T(8,128)(2,1)S(1)}, bf16[2048,128]{1,0:T(8,128)(2,1)S(1)}, u32[]{:S(2)}, u32[]{:S(2)}) collective-permute-start(bf16[2048,128]{1,0:T(8,128)(2,1)S(1)} %collective-permute-done.11), channel_id=1, source_target_pairs={{0,60},{4,0},{8,4},{12,8},{16,12},{20,16},{24,20},{28,24},{32,28},... | collective-permute-start | bytes 1572872 | tf_op jit(solution)/shard_map/ppermute | solution.py:130
  74.0 6.1 %collective-permute-start.14 = (bf16[2048,128]{1,0:T(8,128)(2,1)S(1)}, bf16[2048,128]{1,0:T(8,128)(2,1)S(1)}, u32[]{:S(2)}, u32[]{:S(2)}) collective-permute-start(bf16[2048,128]{1,0:T(8,128)(2,1)S(1)} %collective-permute-done.12), channel_id=1, source_target_pairs={{0,4},{4,8},{8,12},{12,16},{16,20},{20,24},{24,28},{28,32},{32,36}... | collective-permute-start | bytes 1572872 | tf_op jit(solution)/shard_map/ppermute | solution.py:127
  74.9 11.9 %copy-start.4 = (bf16[2048,128]{1,0:T(8,128)(2,1)S(1)}, bf16[2048,128]{1,0:T(8,128)(2,1)}, u32[]{:S(2)}) copy-start(bf16[2048,128]{1,0:T(8,128)(2,1)} %param.13) | copy-start | bytes 1572868
  86.8 6.6 %copy-start.5 = (bf16[2048,128]{1,0:T(8,128)(2,1)S(1)}, bf16[2048,128]{1,0:T(8,128)(2,1)}, u32[]{:S(2)}) copy-start(bf16[2048,128]{1,0:T(8,128)(2,1)} %param.11) | copy-start | bytes 1572868
  130.1 14.2 %all-to-all-start = ((bf16[8,129,128]{2,1,0:T(8,128)(2,1)}), bf16[8,129,128]{2,1,0:T(8,128)(2,1)S(1)}, u32[]{:S(2)}, u32[]{:S(2)}) async-start(bf16[8,129,128]{2,1,0:T(8,128)(2,1)} %broadcast_in_dim.49), calls=%async_computation | async-start | bytes 557056 | tf_op jit(solution)/shard_map/all_to_all | solution.py:12
  148.5 25.2 %all-to-all-start.1 = ((f32[16,1,2048]{2,1,0:T(1,128)}), f32[16,1,2048]{2,1,0:T(1,128)S(1)}, u32[]{:S(2)}, u32[]{:S(2)}) async-start(f32[16,1,2048]{2,1,0:T(1,128)} %broadcast_in_dim.53), calls=%async_computation.1 | async-start | bytes 262144 | tf_op jit(solution)/shard_map/all_to_all | solution.py:12
